TPU v7x, 32 devices: a whole 2x2x4 slice. The times are simulated.
32 devices in a mesh: shuf: 8 (over z, y), rep: 4 (over x, core).
Axes of the slice: x: 2, y: 2, z: 4, core: 2. Of those that a mesh axis runs over, the one named last changes fastest.
Arguments:
- values: bfloat16 [65536, 1024], P('shuf', 'rep')
- subgroup: int32 [512], P('shuf'), may hold values from 0 to 31
- owners: int32 [512, 1], P('shuf'), may hold values from 0 to 7; in each aligned block of 64 rows (0 to 63, 64 to 127, ...) at most 16 rows name the same one
- col_gain: float32 [1024], P('rep'), may hold values from 0.5 to 1.5
- col_bias: float32 [1024], P('rep'), may hold values from -3 to 3
- out_weight: bfloat16 [1024, 1024], P('rep'), may hold values from -0.1875 to 0.1875
Outputs:
- projected: bfloat16 [65536, 1024], P(('shuf', 'rep'))
Inputs may be any that keep to these rules, and one draw needn't show every extreme that they name: `owners`: among the tiles of one index of shuf no owner is named more than 16 times, a bound that some block reaches.
All inputs are finite; a program needn't handle non-finite values.
Results may differ from a plain program's by a relative error of at most 0.015.
Values may be sent and summed in bfloat16 or wider, within the bound.
A program may use at most 64 MiB of HBM per device.

v0:
```python
import jax
import jax.numpy as jnp
from jax import lax
from jax.sharding import PartitionSpec as P

GRP_DEV = 32
PRIOR = 256


def moments(group_sum, group_sq, count, mean_all, square_all):
    weight = (count + float(PRIOR))[:, None]
    center = (group_sum + float(PRIOR) * mean_all) / weight
    second = (group_sq + float(PRIOR) * square_all) / weight
    return (center, lax.rsqrt(second - center * center + 1e-05))


def slot_places(target, capacity, peer_count):
    one_hot = (target[:, None] == jnp.arange(peer_count, dtype=jnp.int32)[None, :]).astype(
        jnp.int32
    )
    position = jnp.sum((jnp.cumsum(one_hot, axis=0) - one_hot) * one_hot, axis=1)
    return target * capacity + position


def on_device(values, subgroup, owners, col_gain, col_bias, out_weight):
    local_rows, local_cols = values.shape
    tile_count = subgroup.shape[0]
    tile_rows = local_rows // tile_count
    peer_count = lax.axis_size("shuf")
    shaped = values.reshape(tile_count, tile_rows, local_cols)
    widened = shaped.astype(jnp.float32)
    tile_sum = jnp.sum(widened, axis=1)
    tile_sq = jnp.sum(widened * widened, axis=1)
    col_sum, col_square = lax.psum((jnp.sum(tile_sum, axis=0), jnp.sum(tile_sq, axis=0)), "shuf")
    row_count = float(local_rows * peer_count)
    mean_all = col_sum / row_count
    square_all = col_square / row_count
    target = owners[:, 0]
    capacity = max(2, 2 * tile_count // peer_count)
    slot_index = slot_places(target, capacity, peer_count)
    packed = jnp.concatenate([tile_sum, tile_sq], axis=1)
    outgoing = (
        jnp.zeros((peer_count * capacity, 2 * local_cols), jnp.float32).at[slot_index].set(packed)
    )
    labels = (
        jnp.full((peer_count * capacity,), -1.0, jnp.float32)
        .at[slot_index]
        .set(subgroup.astype(jnp.float32))
    )
    arrived, arrived_labels = (
        lax.all_to_all(
            outgoing.astype(jnp.bfloat16), "shuf", split_axis=0, concat_axis=0, tiled=True
        ).astype(outgoing.dtype),
        lax.all_to_all(
            labels.astype(jnp.bfloat16), "shuf", split_axis=0, concat_axis=0, tiled=True
        ).astype(labels.dtype),
    )
    group_ids = arrived_labels.astype(jnp.int32)
    members = (group_ids[:, None] == jnp.arange(GRP_DEV, dtype=jnp.int32)[None, :]).astype(
        jnp.float32
    )
    group_sum = jnp.dot(members.T, arrived[:, :local_cols], precision=lax.Precision.HIGHEST)
    group_sq = jnp.dot(members.T, arrived[:, local_cols:], precision=lax.Precision.HIGHEST)
    count = float(tile_rows) * jnp.sum(members, axis=0)
    center, inverse = moments(group_sum, group_sq, count, mean_all, square_all)
    slot_center = jnp.dot(members, center, precision=lax.Precision.HIGHEST)
    slot_inverse = jnp.dot(members, inverse, precision=lax.Precision.HIGHEST)
    back_center, back_inverse = (
        lax.all_to_all(
            slot_center.astype(jnp.bfloat16), "shuf", split_axis=0, concat_axis=0, tiled=True
        ).astype(slot_center.dtype),
        lax.all_to_all(
            slot_inverse.astype(jnp.bfloat16), "shuf", split_axis=0, concat_axis=0, tiled=True
        ).astype(slot_inverse.dtype),
    )
    tile_center = back_center[slot_index]
    tile_scale = back_inverse[slot_index] * col_gain
    scored = ((widened - tile_center[:, None, :]) * tile_scale[:, None, :] + col_bias).astype(
        jnp.bfloat16
    )
    standard = scored.reshape(local_rows, local_cols)
    return lax.psum_scatter(
        jnp.dot(standard, out_weight, preferred_element_type=jnp.float32).astype(jnp.bfloat16),
        "rep",
        scatter_dimension=0,
        tiled=True,
    )


def solution(mesh):
    return jax.shard_map(
        on_device,
        mesh=mesh,
        in_specs=(P("shuf", "rep"), P("shuf"), P("shuf", None), P("rep"), P("rep"), P("rep", None)),
        out_specs=P(("shuf", "rep"), None),
        check_vma=False,
    )
```

profile of v0, /device:TPU:1, one launch (start us, length us, event | category | flops | bytes accessed | tf_op | source)
XLA Modules:
  0.0 227.4 jit_solution(16070103691327121603)
XLA Ops:
  6.5 0.7 convert_element_type.72
  7.3 0.7 fusion.16
  8.1 0.8 select_reduce_fusion
  8.9 0.7 fusion.21
  9.6 0.8 scatter_custom_fusion
  10.4 0.7 all_to_all.35
  11.1 6.4 %all-to-all-start = ((bf16[8,16,1]{1,2,0:T(2,128)(2,1)}), bf16[8,16,1]{1,2,0:T(2,128)(2,1)S(1)}, u32[]{:S(2)}, u32[]{:S(2)}) async-start(bf16[8,16,1]{1,2,0:T(2,128)(2,1)} %all_to_all.35), calls=%async_computation | async-start | bytes 8192 | tf_op jit(solution)/shard_map/all_to_all | solution.py:54
  17.4 3.3 %fusion.2 = (f32[256]{0:T(256)S(1)}, f32[256]{0:T(256)S(1)}) fusion(bf16[8192,256]{1,0:T(8,128)(2,1)} %param.6), kind=kLoop, calls=%fused_computation.13 | loop fusion | flops 8388096 | bytes 4196352 | tf_op jit(solution)/shard_map/reduce_sum | solution.py:34
  20.7 4.6 %bitcast_reduce_fusion = (f32[64,256]{1,0:T(8,128)S(1)}, f32[64,256]{1,0:T(8,128)S(1)}) fusion(bf16[8192,256]{1,0:T(8,128)(2,1)} %param.6), kind=kLoop, calls=%fused_computation.10 | loop fusion | flops 8355840 | bytes 4325376 | tf_op jit(solution)/shard_map/reduce_sum | solution.py:32
  25.4 17.8 %all-reduce = (f32[256]{0:T(256)S(1)}, f32[256]{0:T(256)S(1)}) all-reduce(f32[256]{0:T(256)S(1)} %get-tuple-element.6, f32[256]{0:T(256)S(1)} %get-tuple-element.5), channel_id=1, replica_groups=mesh['shuf'=8,'rep'=4] {'shuf'}, use_global_device_ids=true, to_apply=%region_7.8 | all-reduce | flops 512 | bytes 4096 | tf_op jit(solution)/shard_map/psum | solution.py:34
  43.2 0.9 scatter_custom_fusion.1
  44.1 0.7 convert_element_type.79
  44.8 3.4 %all-to-all-start.1 = ((bf16[8,16,512]{2,1,0:T(8,128)(2,1)}), bf16[8,16,512]{2,1,0:T(8,128)(2,1)S(1)}, u32[]{:S(2)}, u32[]{:S(2)}) async-start(bf16[8,16,512]{2,1,0:T(8,128)(2,1)} %bitcast.4), calls=%async_computation.1 | async-start | bytes 262144 | tf_op jit(solution)/shard_map/all_to_all | solution.py:51
  48.4 5.9 %all-to-all-done.1 = bf16[8,16,512]{2,1,0:T(8,128)(2,1)S(1)} async-done(((bf16[8,16,512]{2,1,0:T(8,128)(2,1)}), bf16[8,16,512]{2,1,0:T(8,128)(2,1)S(1)}, u32[]{:S(2)}, u32[]{:S(2)}) %all-to-all-start.1) | async-done | bytes 131104 | tf_op jit(solution)/shard_map/all_to_all | solution.py:51
  54.6 0.9 convolution_convert_fusion.1
  55.5 3.4 %all-to-all-start.3 = ((bf16[8,16,256]{2,1,0:T(8,128)(2,1)}), bf16[8,16,256]{2,1,0:T(8,128)(2,1)S(1)}, u32[]{:S(2)}, u32[]{:S(2)}) async-start(bf16[8,16,256]{2,1,0:T(8,128)(2,1)} %bitcast.9), calls=%async_computation.3 | async-start | bytes 131072 | tf_op jit(solution)/shard_map/all_to_all | solution.py:72
  58.8 0.9 convolution_convert_fusion.2
  59.7 4.8 %all-to-all-done.3 = bf16[8,16,256]{2,1,0:T(8,128)(2,1)S(1)} async-done(((bf16[8,16,256]{2,1,0:T(8,128)(2,1)}), bf16[8,16,256]{2,1,0:T(8,128)(2,1)S(1)}, u32[]{:S(2)}, u32[]{:S(2)}) %all-to-all-start.3) | async-done | bytes 65568 | tf_op jit(solution)/shard_map/all_to_all | solution.py:72
  64.5 3.3 %all-to-all-start.2 = ((bf16[8,16,256]{2,1,0:T(8,128)(2,1)}), bf16[8,16,256]{2,1,0:T(8,128)(2,1)S(1)}, u32[]{:S(2)}, u32[]{:S(2)}) async-start(bf16[8,16,256]{2,1,0:T(8,128)(2,1)} %bitcast.6), calls=%async_computation.2 | async-start | bytes 131072 | tf_op jit(solution)/shard_map/all_to_all | solution.py:69
  68.6 5.0 %all-to-all-done.2 = bf16[8,16,256]{2,1,0:T(8,128)(2,1)S(1)} async-done(((bf16[8,16,256]{2,1,0:T(8,128)(2,1)}), bf16[8,16,256]{2,1,0:T(8,128)(2,1)S(1)}, u32[]{:S(2)}, u32[]{:S(2)}) %all-to-all-start.2) | async-done | bytes 65568 | tf_op jit(solution)/shard_map/all_to_all | solution.py:69
  73.6 0.7 gather_fusion
  74.3 5.6 %fusion.1 = bf16[8192,256]{1,0:T(8,128)(2,1)} fusion(bf16[8192,256]{1,0:T(8,128)(2,1)} %param.6, f32[256]{0:T(256)S(1)} %copy-done.2, f32[64,256]{1,0:T(8,128)S(1)} %broadcast_multiply_fusion, f32[64,256]{1,0:T(8,128)S(1)} %gather_fusion), kind=kLoop, calls=%fused_computation.7 | loop fusion | flops 10485760 | bytes 8520704 | tf_op jit(solution)/shard_map/convert_element_type | solution.py:78
  79.9 10.4 %convolution_convert_fusion = bf16[8192,1024]{1,0:T(8,128)(2,1)} fusion(bf16[8192,256]{1,0:T(8,128)(2,1)} %fusion.1, bf16[256,1024]{1,0:T(8,128)(2,1)S(1)} %copy-done), kind=kOutput, calls=%fused_computation.4 | convolution fusion | flops 4303355904 | bytes 21495808 | tf_op jit(solution)/shard_map/dot_general | solution.py:83
  90.3 130.3 %reduce-scatter.2.cloned.1.call-done = bf16[2048,1024]{1,0:T(8,128)(2,1)} async-done(((bf16[8192,1024]{1,0:T(8,128)(2,1)}), bf16[2048,1024]{1,0:T(8,128)(2,1)}) %reduce-scatter.2.cloned.1.call-update) | async-done | bytes 4194320 | tf_op jit(solution)/shard_map/reduce_scatter | solution.py:82
  (23 shorter events, 1.4 us)
Async XLA Ops:
  6.5 73.3 %copy-start = (bf16[256,1024]{1,0:T(8,128)(2,1)S(1)}, bf16[256,1024]{1,0:T(8,128)(2,1)}, u32[]{:S(2)}) copy-start(bf16[256,1024]{1,0:T(8,128)(2,1)} %param.11) | copy-start | bytes 1572868
  6.5 67.7 %copy-start.1 = (f32[256]{0:T(256)S(1)}, f32[256]{0:T(256)}, u32[]{:S(2)}) copy-start(f32[256]{0:T(256)} %param.9) | copy-start | bytes 3076
  6.5 67.7 %copy-start.2 = (f32[256]{0:T(256)S(1)}, f32[256]{0:T(256)}, u32[]{:S(2)}) copy-start(f32[256]{0:T(256)} %param.10) | copy-start | bytes 3076
  11.1 33.7 %all-to-all-start = ((bf16[8,16,1]{1,2,0:T(2,128)(2,1)}), bf16[8,16,1]{1,2,0:T(2,128)(2,1)S(1)}, u32[]{:S(2)}, u32[]{:S(2)}) async-start(bf16[8,16,1]{1,2,0:T(2,128)(2,1)} %all_to_all.35), calls=%async_computation | async-start | bytes 8192 | tf_op jit(solution)/shard_map/all_to_all | solution.py:54
  44.8 9.5 %all-to-all-start.1 = ((bf16[8,16,512]{2,1,0:T(8,128)(2,1)}), bf16[8,16,512]{2,1,0:T(8,128)(2,1)S(1)}, u32[]{:S(2)}, u32[]{:S(2)}) async-start(bf16[8,16,512]{2,1,0:T(8,128)(2,1)} %bitcast.4), calls=%async_computation.1 | async-start | bytes 262144 | tf_op jit(solution)/shard_map/all_to_all | solution.py:51
  55.5 9.1 %all-to-all-start.3 = ((bf16[8,16,256]{2,1,0:T(8,128)(2,1)}), bf16[8,16,256]{2,1,0:T(8,128)(2,1)S(1)}, u32[]{:S(2)}, u32[]{:S(2)}) async-start(bf16[8,16,256]{2,1,0:T(8,128)(2,1)} %bitcast.9), calls=%async_computation.3 | async-start | bytes 131072 | tf_op jit(solution)/shard_map/all_to_all | solution.py:72
  64.5 9.0 %all-to-all-start.2 = ((bf16[8,16,256]{2,1,0:T(8,128)(2,1)}), bf16[8,16,256]{2,1,0:T(8,128)(2,1)S(1)}, u32[]{:S(2)}, u32[]{:S(2)}) async-start(bf16[8,16,256]{2,1,0:T(8,128)(2,1)} %bitcast.6), calls=%async_computation.2 | async-start | bytes 131072 | tf_op jit(solution)/shard_map/all_to_all | solution.py:69
  67.9 152.7 %reduce-scatter.2.cloned.1.call-start = ((), (), s32[]{:S(2)}) async-start(), calls=%async_computation.5 | async-start | bytes 20971520 | tf_op jit(solution)/shard_map/reduce_scatter | solution.py:82
Sparse Core Ops, SparseCore 0:
  90.4 130.0 reduce-scatter.1
where the time goes:
time: 229 us; the launch traced here: 227 us
  waiting for transfers between devices  146 us (64%)
  other arithmetic  18.3 us (8%)
  blocking collectives  17.8 us (8%)
  starting transfers between devices  16.5 us (7%)
  between operations  13.5 us (6%)
  matrix products  12.5 us (5%)
  local copies, waits for them, and re-layouts  2.85 us (1%)
    reduce_scatter x1, waiting for transfers between devices, on_device(): lax.psum_scatter(jnp.dot(standard, out_weight, preferred_element_type=jnp...  130 us
    psum x1, blocking collectives, on_device(): lax.psum((jnp.sum(tile_sum, axis=0), jnp.sum(tile_sq, axis=0)), 'shuf')  17.8 us
    dot_general x1, matrix products, on_device(): jnp.dot(standard, out_weight, preferred_element_type=jnp.float32)  10.4 us
    all_to_all x1, starting transfers between devices, on_device(): lax.all_to_all(labels.astype(jnp.bfloat16), 'shuf', split_axis=0, concat_...  6.37 us
    all_to_all x1, waiting for transfers between devices, on_device(): lax.all_to_all(outgoing.astype(jnp.bfloat16), 'shuf', split_axis=0, conca...  5.9 us
    convert_element_type x1, other arithmetic, on_device(): ((widened - tile_center[:, None, :]) * tile_scale[:, None, :] + col_bias)...  5.57 us
    all_to_all x1, waiting for transfers between devices, on_device(): lax.all_to_all(slot_center.astype(jnp.bfloat16), 'shuf', split_axis=0, co...  4.96 us
    all_to_all x1, waiting for transfers between devices, on_device(): lax.all_to_all(slot_inverse.astype(jnp.bfloat16), 'shuf', split_axis=0, c...  4.8 us
  transfers between devices with their start and end apart: 5, of which 4 were waited for; matrix products, arithmetic and copies ran while one was open for 5% of the time, Pallas kernels for 0%

commit v1 on v0

v1 whole, which is shorter than its diff:
```python
import functools
import math

import jax
import jax.numpy as jnp
from jax import lax
from jax.experimental import pallas as pl
from jax.experimental.pallas import tpu as pltpu
from jax.sharding import PartitionSpec as P

GRP_DEV = 32
PRIOR = 256
EPS = 1e-05
EXTRA = 8
CHUNKS = 8
FIRST = 5
LOADS = 8
MESH = pl.DeviceIdType.MESH


def kernel(
    shuf_size,
    rep_size,
    values,
    weight,
    gid_cols,
    gid_rows,
    gain,
    bias,
    out,
    held,
    arrived,
    packets,
    weights,
    stats_out,
    stats_in,
    scored,
    load_sem,
    own_sem,
    val_send,
    val_recv,
    pack_send,
    pack_recv,
    fwd_send,
    fwd_recv,
    wx_send,
    wx_recv,
    wg_send,
    wg_recv,
    wf_send,
    wf_recv,
    wn_send,
    wn_recv,
    st_send,
    st_recv,
):
    shuf, rep = lax.axis_index("shuf"), lax.axis_index("rep")
    half = rep_size // 2
    outer = shuf_size // 2
    slices = weights.shape[2]
    slice_outer = slices // 2
    local_rows, cols = values.shape
    block_rows = local_rows // rep_size
    tiles = gid_cols.shape[0] - EXTRA
    tile_rows = local_rows // tiles
    block_tiles = tiles // rep_size
    chunk = block_rows // CHUNKS
    high, low = rep // half, rep % half
    s_out, s_in = shuf // 2, shuf % 2
    mate = s_out * 2 + 1 - s_in
    cut = shuf % slices
    cut_base = shuf - cut
    cut_out = cut // 2

    def rep_peer(dh, dl):
        return ((high + dh) % 2) * half + (low + dl) % half

    def outer_peer(e):
        return ((s_out + e) % outer) * 2 + s_in

    def cut_peer(e):
        return cut_base + ((cut_out + e) % slice_outer) * 2 + s_in

    rep_offsets = [(dh, dl) for dh in range(2) for dl in range(half) if (dh, dl) != (0, 0)]

    def remote(src, dst, send, recv, s, k):
        return pltpu.make_async_remote_copy(
            src_ref=src, dst_ref=dst, send_sem=send, recv_sem=recv,
            device_id=(s, k), device_id_type=MESH,
        )

    def value_copy(dh, dl, ch):
        peer = rep_peer(dh, dl)
        slot = dh * half + dl
        start = pl.multiple_of(peer * block_rows + ch * chunk, chunk)
        return remote(
            values.at[pl.ds(start, chunk)],
            arrived.at[slot, pl.ds(ch * chunk, chunk)],
            val_send.at[slot, ch], val_recv.at[slot, ch], shuf, peer,
        )

    def load_copy(i):
        size = local_rows // LOADS
        return pltpu.make_async_copy(
            values.at[pl.ds(i * size, size)], held.at[pl.ds(i * size, size)], load_sem.at[i]
        )

    own_weight = pltpu.make_async_copy(weight, weights.at[0, 0], own_sem)
    for i in range(LOADS):
        load_copy(i).start()
    own_weight.start()

    barrier = pltpu.get_barrier_semaphore()
    peers = [(shuf, rep_peer(dh, dl)) for dh, dl in rep_offsets]
    peers += [(mate, rep)] + [(outer_peer(e), rep) for e in range(1, outer)]
    for s, k in peers:
        pl.semaphore_signal(barrier, inc=1, device_id=(s, k), device_id_type=MESH)
    pl.semaphore_wait(barrier, len(peers))

    wx = remote(weight.at[cut], weights.at[1, 0, cut], wx_send, wx_recv, shuf, rep_peer(1, 0))
    wx.start()
    far = [(1, dl) for dl in range(half)]
    near = [(0, dl) for dl in range(1, half)]
    for ch in range(FIRST):
        for dh, dl in far:
            value_copy(dh, dl, ch).start()
    for ch in range(CHUNKS):
        for dh, dl in near:
            value_copy(dh, dl, ch).start()

    packets[0, 0, tiles:, :] = gid_rows[...]
    group = 8
    per_load = tiles // LOADS
    for i in range(LOADS):
        load_copy(i).wait()

        def sums(g, carry):
            first = pl.multiple_of(i * per_load + g * group, group)
            parts, squares = [], []
            for u in range(group):
                x = held[pl.ds(pl.multiple_of((first + u) * tile_rows, tile_rows), tile_rows), :]
                x = x.astype(jnp.float32)
                parts.append(jnp.sum(x, axis=0, keepdims=True))
                squares.append(jnp.sum(x * x, axis=0, keepdims=True))
            packets[0, 0, pl.ds(first, group), :cols] = jnp.concatenate(parts, axis=0)
            packets[0, 0, pl.ds(first, group), cols:] = jnp.concatenate(squares, axis=0)
            return carry

        lax.fori_loop(0, per_load // group, sums, 0)

    def pack_copy(e):
        return remote(
            packets.at[0, 0], packets.at[0, e], pack_send.at[e], pack_recv.at[e], outer_peer(e), rep
        )

    def fwd_copy(e):
        return remote(
            packets.at[0, e], packets.at[1, e], fwd_send.at[e], fwd_recv.at[e], mate, rep
        )

    def cut_copy(e):
        here = weights.at[1, 0, cut]
        return remote(here, here, wg_send.at[e], wg_recv.at[e], cut_peer(e), rep)

    def cut_forward(e):
        index = ((cut_out + slice_outer - e) % slice_outer) * 2 + s_in
        there = weights.at[1, 0, index]
        return remote(there, there, wf_send.at[e], wf_recv.at[e], mate, rep)

    for e in range(1, outer):
        pack_copy(e).start()
    fwd_copy(0).start()
    wx.wait_recv()
    for e in range(1, slice_outer):
        cut_copy(e).start()

    def members(i, e):
        same = gid_cols[...] == packets[i, e, tiles:tiles + 1, :tiles]
        row = lax.broadcasted_iota(jnp.int32, (tiles + EXTRA, tiles), 0)
        return jnp.where(same | (row >= tiles), 1.0, 0.0).astype(jnp.float32)

    def gathered(i, e):
        m = members(i, e)
        part = jnp.dot(
            m, packets[i, e, :tiles, :],
            precision=lax.Precision.HIGHEST, preferred_element_type=jnp.float32,
        )
        return part, jnp.sum(m, axis=1, keepdims=True)

    total, count = gathered(0, 0)
    for e in range(1, outer):
        pack_copy(e).wait_recv()
        fwd_copy(e).start()
        part, number = gathered(0, e)
        total, count = total + part, count + number
    cut_forward(0).start()
    for e in range(1, slice_outer):
        cut_copy(e).wait_recv()
        cut_forward(e).start()
    for e in range(outer):
        fwd_copy(e).wait_recv()
        part, number = gathered(1, e)
        total, count = total + part, count + number

    row_count = float(local_rows * shuf_size)
    overall = total[tiles:tiles + 1] / row_count
    weight_sum = count[:tiles] * float(tile_rows) + float(PRIOR)
    pooled = (total[:tiles] + float(PRIOR) * overall) / weight_sum
    center, second = pooled[:, :cols], pooled[:, cols:]
    scale = lax.rsqrt(second - center * center + EPS) * gain[...]
    offset = bias[...] - center * scale
    for j in range(rep_size):
        stats_out[j, 0] = scale[j * block_tiles:(j + 1) * block_tiles]
        stats_out[j, 1] = offset[j * block_tiles:(j + 1) * block_tiles]

    def stat_copy(dh, dl):
        peer = rep_peer(dh, dl)
        slot = dh * half + dl
        return remote(
            stats_out.at[peer], stats_in.at[slot], st_send.at[slot], st_recv.at[slot], shuf, peer
        )

    for dh, dl in reversed(rep_offsets):
        stat_copy(dh, dl).start()
    for ch in range(FIRST, CHUNKS):
        for dh, dl in far:
            value_copy(dh, dl, ch).start()
    stats_in[0] = stats_out[rep]

    own_weight.wait()
    for e in range(slice_outer):
        cut_forward(e).wait_recv()

    def near_copy(dh, dl):
        return remote(
            weights.at[dh, 0], weights.at[dh, dl],
            wn_send.at[dh, dl], wn_recv.at[dh, dl], shuf, rep_peer(0, dl),
        )

    for dl in range(1, half):
        for dh in range(2):
            near_copy(dh, dl).start()
    for dh, dl in rep_offsets:
        stat_copy(dh, dl).wait_recv()
    for dl in range(1, half):
        for dh in range(2):
            near_copy(dh, dl).wait_recv()

    def project(ch, carry):
        for dh, dl in rep_offsets:
            value_copy(dh, dl, ch).wait_recv()
        for slot in range(rep_size):
            for u in range(chunk // tile_rows):
                tile = ch * (chunk // tile_rows) + u
                at = ch * chunk + u * tile_rows
                if slot == 0:
                    start = pl.multiple_of(rep * block_rows + at, tile_rows)
                    x = held[pl.ds(start, tile_rows), :]
                else:
                    x = arrived[slot, pl.ds(pl.multiple_of(at, tile_rows), tile_rows), :]
                s = stats_in[slot, 0, pl.ds(tile, 1), :]
                t = stats_in[slot, 1, pl.ds(tile, 1), :]
                scored[u * tile_rows:(u + 1) * tile_rows, slot * cols:(slot + 1) * cols] = (
                    x.astype(jnp.float32) * s + t
                ).astype(jnp.bfloat16)
        whole = weights[...].reshape(rep_size * cols, weights.shape[-1])
        out[pl.ds(pl.multiple_of(ch * chunk, chunk), chunk), :] = jnp.dot(
            scored[...], whole, preferred_element_type=jnp.float32
        ).astype(out.dtype)
        return carry

    lax.fori_loop(0, CHUNKS, project, 0)

    wx.wait_send()
    for ch in range(CHUNKS):
        for dh, dl in rep_offsets:
            value_copy(dh, dl, ch).wait_send()
    for e in range(1, outer):
        pack_copy(e).wait_send()
    for e in range(outer):
        fwd_copy(e).wait_send()
    for e in range(1, slice_outer):
        cut_copy(e).wait_send()
    for e in range(slice_outer):
        cut_forward(e).wait_send()
    for dh, dl in rep_offsets:
        stat_copy(dh, dl).wait_send()
    for dl in range(1, half):
        for dh in range(2):
            near_copy(dh, dl).wait_send()


def on_device(shuf_size, rep_size, values, subgroup, owners, col_gain, col_bias, out_weight):
    local_rows, cols = values.shape
    tiles = subgroup.shape[0]
    outs = out_weight.shape[1]
    group = (owners[:, 0] * GRP_DEV + subgroup).astype(jnp.float32)
    gid_cols = jnp.broadcast_to(
        jnp.pad(group, (0, EXTRA), constant_values=-1.0)[:, None], (tiles + EXTRA, tiles)
    )
    gid_rows = jnp.broadcast_to(
        jnp.pad(group, (0, 2 * cols - tiles), constant_values=-2.0)[None, :], (EXTRA, 2 * cols)
    )
    slices = math.gcd(shuf_size, cols // 32)
    outer, half, slice_outer = shuf_size // 2, rep_size // 2, slices // 2
    block_rows = local_rows // rep_size
    chunk = block_rows // CHUNKS
    f32, bf16 = jnp.float32, jnp.bfloat16
    dma = pltpu.SemaphoreType.DMA
    vmem = pl.BlockSpec(memory_space=pltpu.VMEM)
    anywhere = pl.BlockSpec(memory_space=pl.ANY)
    return pl.pallas_call(
        functools.partial(kernel, shuf_size, rep_size),
        out_shape=jax.ShapeDtypeStruct((block_rows, outs), bf16),
        in_specs=[anywhere, anywhere, vmem, vmem, vmem, vmem],
        out_specs=vmem,
        scratch_shapes=[
            pltpu.VMEM((local_rows, cols), bf16),
            pltpu.VMEM((rep_size, block_rows, cols), bf16),
            pltpu.VMEM((2, outer, tiles + EXTRA, 2 * cols), f32),
            pltpu.VMEM((2, half, slices, cols // slices, outs), bf16),
            pltpu.VMEM((rep_size, 2, tiles // rep_size, cols), f32),
            pltpu.VMEM((rep_size, 2, tiles // rep_size, cols), f32),
            pltpu.VMEM((chunk, rep_size * cols), bf16),
            dma((LOADS,)),
            dma,
            dma((rep_size, CHUNKS)),
            dma((rep_size, CHUNKS)),
            dma((outer,)),
            dma((outer,)),
            dma((outer,)),
            dma((outer,)),
            dma,
            dma,
            dma((slice_outer,)),
            dma((slice_outer,)),
            dma((slice_outer,)),
            dma((slice_outer,)),
            dma((2, half)),
            dma((2, half)),
            dma((rep_size,)),
            dma((rep_size,)),
        ],
        compiler_params=pltpu.CompilerParams(collective_id=0, has_side_effects=True),
    )(
        values,
        out_weight.reshape(slices, cols // slices, outs),
        gid_cols,
        gid_rows,
        col_gain[None, :],
        col_bias[None, :],
    )


def solution(mesh):
    return jax.shard_map(
        functools.partial(on_device, mesh.shape["shuf"], mesh.shape["rep"]),
        mesh=mesh,
        in_specs=(P("shuf", "rep"), P("shuf"), P("shuf", None), P("rep"), P("rep"), P("rep", None)),
        out_specs=P(("shuf", "rep"), None),
        check_vma=False,
    )
```

time: 229 us -> 65.7 us (0.29)
  waiting for transfers between devices: 146 us -> 0 us
  Pallas kernels: 0 us -> 58.9 us
  blocking collectives: 17.8 us -> 0 us
  other arithmetic: 18.3 us -> 0.68 us
  starting transfers between devices: 16.5 us -> 0 us
  between operations: 13.5 us -> 0.01 us
  matrix products: 12.5 us -> 0 us
  local copies, waits for them, and re-layouts: 2.85 us -> 5.94 us
    reduce_scatter x1 -> x0, waiting for transfers between devices: 130 us -> none  [on_device(): lax.psum_scatter(jnp.dot(standard, out_weight, preferred_element_type=jnp...]
    pallas_call x0 -> x1, Pallas kernels: none -> 58.9 us  [on_device(): pl.pallas_call(functools.partial(kernel, shuf_size, rep_size), out_shape=...]
    psum x1 -> x0, blocking collectives: 17.8 us -> none  [on_device(): lax.psum((jnp.sum(tile_sum, axis=0), jnp.sum(tile_sq, axis=0)), 'shuf')]
    all_to_all x4 -> x0, starting transfers between devices: 16.4 us -> none  [the longest x1 6.37 us: on_device(): lax.all_to_all(labels.astype(jnp.bfloat16), 'shuf', split_axis=0, concat_...]
    all_to_all x4 -> x0, waiting for transfers between devices: 15.7 us -> none  [the longest x1 5.9 us: on_device(): lax.all_to_all(outgoing.astype(jnp.bfloat16), 'shuf', split_axis=0, conca...]
    dot_general x5 -> x0, matrix products: 12.5 us -> none  [the longest x1 10.4 us: on_device(): jnp.dot(standard, out_weight, preferred_element_type=jnp.float32)]
    reduce_sum x4 -> x0, other arithmetic: 8.9 us -> none  [the longest x1 4.64 us: on_device(): tile_sum = jnp.sum(widened, axis=1)]
    convert_element_type x8 -> x1, other arithmetic: 7.74 us -> 0.68 us  [on_device(): group = (owners[:, 0] * GRP_DEV + subgroup).astype(jnp.float32)]
  transfers between devices with their start and end apart: 5 -> 0, of which waited for: 4 -> 0; matrix products, arithmetic and copies ran while one was open for 5% -> 0% of each run, Pallas kernels for 0% -> 0%
where the time goes in v1:
time: 65.7 us; the launch traced here: 65.5 us
  Pallas kernels  58.9 us (90%)
  local copies, waits for them, and re-layouts  5.94 us (9%)
  other arithmetic  0.68 us (1%)
    pallas_call x1, Pallas kernels, on_device(): pl.pallas_call(functools.partial(kernel, shuf_size, rep_size), out_shape=...  58.9 us
    unnamed x1, local copies, waits for them, and re-layouts  4.64 us

profile of v1, /device:TPU:1, one launch (start us, length us, event | category | flops | bytes accessed | tf_op | source)
XLA Modules:
  0.0 65.5 jit_solution(714332806870872056)
XLA Ops:
  0.0 0.7 %fusion = f32[64]{0:T(128)S(1)} fusion(s32[64]{0:T(128)} %param.7, s32[64,1]{0,1:T(1,128)} %param.8), kind=kLoop, calls=%fused_computation.1 | loop fusion | flops 192 | bytes 768 | tf_op jit(solution)/shard_map/convert_element_type | solution.py:297
  0.7 0.6 broadcast_in_dim.9.gid_rows
  1.3 0.7 %broadcast_in_dim.8.gid_cols = f32[72,64]{1,0:T(8,128)} broadcast(f32[72]{0:T(128)S(1)} %pad.8), dimensions={0} | broadcast | bytes 18720 | tf_op jit(solution)/shard_map/broadcast_in_dim | solution.py:298
  2.0 58.9 %shard_map.64 = bf16[2048,1024]{1,0:T(8,128)(2,1)} custom-call(bf16[8192,256]{1,0:T(8,128)(2,1)} %values.1, bf16[8,32,1024]{2,1,0:T(8,128)(2,1)} %bitcast.7, f32[72,64]{1,0:T(8,128)} %broadcast_in_dim.8.gid_cols, f32[8,512]{1,0:T(8,128)} %broadcast_in_dim.9.gid_rows, f32[1,256]{1,0:T(1,128)} %bitcast.8, f32[1,256]{1,0:T(1,128)} %bitcast.9), custom_call_target="tpu_custom_call" | custom-call | tf_op jit(solution)/shard_map/pallas_call | solution.py:312
  60.8 4.6 %copy.8 = bf16[2048,1024]{1,0:T(8,128)(2,1)} copy(bf16[2048,1024]{1,0:T(8,128)(2,1)} %shard_map.64) | data formatting | bytes 8388608
  (2 shorter events, 0.0 us)

commit v2 on v1

--- a/solution.py
+++ b/solution.py
@@ -15,6 +15,7 @@
 CHUNKS = 8
 FIRST = 5
 LOADS = 8
+LIMIT = 59 * 1024 * 1024
 MESH = pl.DeviceIdType.MESH
 
 
@@ -23,8 +24,8 @@
     rep_size,
     values,
     weight,
-    gid_cols,
-    gid_rows,
+    owner,
+    member,
     gain,
     bias,
     out,
@@ -61,7 +62,7 @@
     slice_outer = slices // 2
     local_rows, cols = values.shape
     block_rows = local_rows // rep_size
-    tiles = gid_cols.shape[0] - EXTRA
+    tiles = member.shape[1]
     tile_rows = local_rows // tiles
     block_tiles = tiles // rep_size
     chunk = block_rows // CHUNKS
@@ -128,7 +129,12 @@
         for dh, dl in near:
             value_copy(dh, dl, ch).start()
 
-    packets[0, 0, tiles:, :] = gid_rows[...]
+    gid_row = (owner[...] * GRP_DEV + member[...]).astype(jnp.float32)
+    packets[0, 0, tiles:tiles + 1, :tiles] = gid_row
+    square = (tiles, tiles)
+    on_diagonal = lax.broadcasted_iota(jnp.int32, square, 0) == lax.broadcasted_iota(jnp.int32, square, 1)
+    gid_col = jnp.sum(jnp.where(on_diagonal, gid_row, 0.0), axis=1, keepdims=True)
+    gid_col = jnp.concatenate([gid_col, jnp.full((EXTRA, 1), -1.0, jnp.float32)], axis=0)
     group = 8
     per_load = tiles // LOADS
     for i in range(LOADS):
@@ -175,7 +181,7 @@
         cut_copy(e).start()
 
     def members(i, e):
-        same = gid_cols[...] == packets[i, e, tiles:tiles + 1, :tiles]
+        same = gid_col == packets[i, e, tiles:tiles + 1, :tiles]
         row = lax.broadcasted_iota(jnp.int32, (tiles + EXTRA, tiles), 0)
         return jnp.where(same | (row >= tiles), 1.0, 0.0).astype(jnp.float32)
 
@@ -294,13 +300,6 @@
     local_rows, cols = values.shape
     tiles = subgroup.shape[0]
     outs = out_weight.shape[1]
-    group = (owners[:, 0] * GRP_DEV + subgroup).astype(jnp.float32)
-    gid_cols = jnp.broadcast_to(
-        jnp.pad(group, (0, EXTRA), constant_values=-1.0)[:, None], (tiles + EXTRA, tiles)
-    )
-    gid_rows = jnp.broadcast_to(
-        jnp.pad(group, (0, 2 * cols - tiles), constant_values=-2.0)[None, :], (EXTRA, 2 * cols)
-    )
     slices = math.gcd(shuf_size, cols // 32)
     outer, half, slice_outer = shuf_size // 2, rep_size // 2, slices // 2
     block_rows = local_rows // rep_size
@@ -308,11 +307,11 @@
     f32, bf16 = jnp.float32, jnp.bfloat16
     dma = pltpu.SemaphoreType.DMA
     vmem = pl.BlockSpec(memory_space=pltpu.VMEM)
-    anywhere = pl.BlockSpec(memory_space=pl.ANY)
+    hbm = pl.BlockSpec(memory_space=pltpu.HBM)
     return pl.pallas_call(
         functools.partial(kernel, shuf_size, rep_size),
-        out_shape=jax.ShapeDtypeStruct((block_rows, outs), bf16),
-        in_specs=[anywhere, anywhere, vmem, vmem, vmem, vmem],
+        out_shape=pltpu.VMEM((block_rows, outs), bf16),
+        in_specs=[hbm, hbm, vmem, vmem, vmem, vmem],
         out_specs=vmem,
         scratch_shapes=[
             pltpu.VMEM((local_rows, cols), bf16),
@@ -341,12 +340,14 @@
             dma((rep_size,)),
             dma((rep_size,)),
         ],
-        compiler_params=pltpu.CompilerParams(collective_id=0, has_side_effects=True),
+        compiler_params=pltpu.CompilerParams(
+            collective_id=0, has_side_effects=True, vmem_limit_bytes=LIMIT
+        ),
     )(
         values,
         out_weight.reshape(slices, cols // slices, outs),
-        gid_cols,
-        gid_rows,
+        owners.reshape(1, tiles),
+        subgroup.reshape(1, tiles),
         col_gain[None, :],
         col_bias[None, :],
     )

time: 65.7 us -> 59.1 us (0.90)
  local copies, waits for them, and re-layouts: 5.94 us -> 2.02 us
  Pallas kernels: 58.9 us -> 56.9 us
  other arithmetic: 0.68 us -> 0 us
    unnamed x1, local copies, waits for them, and re-layouts: 4.64 us -> 2.02 us
    pallas_call x1, Pallas kernels: 58.9 us -> 56.9 us  [on_device(): pl.pallas_call(functools.partial(kernel, shuf_size, rep_size), out_shape=...]
    broadcast_in_dim x2 -> x0, local copies, waits for them, and re-layouts: 1.29 us -> none  [the longest x1 0.69 us: on_device(): jnp.broadcast_to(jnp.pad(group, (0, EXTRA), constant_values=-1.0)[:, None...]
    convert_element_type x1 -> x0, other arithmetic: 0.68 us -> none  [on_device(): group = (owners[:, 0] * GRP_DEV + subgroup).astype(jnp.float32)]
where the time goes in v2:
time: 59.1 us; the launch traced here: 58.9 us
  Pallas kernels  56.9 us (96%)
  local copies, waits for them, and re-layouts  2.02 us (3%)
    pallas_call x1, Pallas kernels, on_device(): pl.pallas_call(functools.partial(kernel, shuf_size, rep_size), out_shape=...  56.9 us
    unnamed x1, local copies, waits for them, and re-layouts  2.02 us

profile of v2, /device:TPU:1, one launch (start us, length us, event | category | flops | bytes accessed | tf_op | source)
XLA Modules:
  0.0 58.9 jit_solution(14618312815008073904)
XLA Ops:
  0.0 56.9 %shard_map.64 = bf16[2048,1024]{1,0:T(8,128)(2,1)S(1)} custom-call(bf16[8192,256]{1,0:T(8,128)(2,1)} %values.1, bf16[8,32,1024]{2,1,0:T(8,128)(2,1)} %bitcast.5, s32[1,64]{1,0:T(1,128)} %bitcast.8, s32[1,64]{1,0:T(1,128)} %bitcast.9, f32[1,256]{1,0:T(1,128)} %bitcast.6, f32[1,256]{1,0:T(1,128)} %bitcast.7), custom_call_target="tpu_custom_call" | custom-call | tf_op jit(solution)/shard_map/pallas_call | solution.py:311
  56.9 2.0 %copy.8 = bf16[2048,1024]{1,0:T(8,128)(2,1)} copy(bf16[2048,1024]{1,0:T(8,128)(2,1)S(1)} %shard_map.64) | data formatting | bytes 8388608

commit v3 on v2

--- a/solution.py
+++ b/solution.py
@@ -15,7 +15,8 @@
 CHUNKS = 8
 FIRST = 5
 LOADS = 8
-LIMIT = 59 * 1024 * 1024
+LIMIT = 58900 * 1024
+LIMIT_LAST = 8 * 1024 * 1024
 MESH = pl.DeviceIdType.MESH
 
 
@@ -29,10 +30,11 @@
     gain,
     bias,
     out,
+    last_scored,
+    weights,
     held,
     arrived,
     packets,
-    weights,
     stats_out,
     stats_in,
     scored,
@@ -252,10 +254,10 @@
         for dh in range(2):
             near_copy(dh, dl).wait_recv()
 
-    def project(ch, carry):
-        for dh, dl in rep_offsets:
-            value_copy(dh, dl, ch).wait_recv()
+    def score(ch, dst):
         for slot in range(rep_size):
+            if slot > 0:
+                value_copy(slot // half, slot % half, ch).wait_recv()
             for u in range(chunk // tile_rows):
                 tile = ch * (chunk // tile_rows) + u
                 at = ch * chunk + u * tile_rows
@@ -266,16 +268,20 @@
                     x = arrived[slot, pl.ds(pl.multiple_of(at, tile_rows), tile_rows), :]
                 s = stats_in[slot, 0, pl.ds(tile, 1), :]
                 t = stats_in[slot, 1, pl.ds(tile, 1), :]
-                scored[u * tile_rows:(u + 1) * tile_rows, slot * cols:(slot + 1) * cols] = (
+                dst[u * tile_rows:(u + 1) * tile_rows, slot * cols:(slot + 1) * cols] = (
                     x.astype(jnp.float32) * s + t
                 ).astype(jnp.bfloat16)
+
+    def project(ch, carry):
+        score(ch, scored)
         whole = weights[...].reshape(rep_size * cols, weights.shape[-1])
         out[pl.ds(pl.multiple_of(ch * chunk, chunk), chunk), :] = jnp.dot(
             scored[...], whole, preferred_element_type=jnp.float32
         ).astype(out.dtype)
         return carry
 
-    lax.fori_loop(0, CHUNKS, project, 0)
+    lax.fori_loop(0, CHUNKS - 1, project, 0)
+    score(CHUNKS - 1, last_scored)
 
     wx.wait_send()
     for ch in range(CHUNKS):
@@ -296,6 +302,26 @@
             near_copy(dh, dl).wait_send()
 
 
+def finish(early, scored, weights, out, tail, sems):
+    rows, last = early.shape[0], scored.shape[0]
+    size = rows // (CHUNKS - 1)
+
+    def early_copy(i):
+        return pltpu.make_async_copy(
+            early.at[pl.ds(i * size, size)], out.at[pl.ds(i * size, size)], sems.at[i]
+        )
+
+    for i in range(CHUNKS - 1):
+        early_copy(i).start()
+    whole = weights[...].reshape(scored.shape[1], weights.shape[-1])
+    tail[...] = jnp.dot(scored[...], whole, preferred_element_type=jnp.float32).astype(tail.dtype)
+    tail_copy = pltpu.make_async_copy(tail, out.at[pl.ds(rows, last)], sems.at[CHUNKS - 1])
+    tail_copy.start()
+    for i in range(CHUNKS - 1):
+        early_copy(i).wait()
+    tail_copy.wait()
+
+
 def on_device(shuf_size, rep_size, values, subgroup, owners, col_gain, col_bias, out_weight):
     local_rows, cols = values.shape
     tiles = subgroup.shape[0]
@@ -308,16 +334,19 @@
     dma = pltpu.SemaphoreType.DMA
     vmem = pl.BlockSpec(memory_space=pltpu.VMEM)
     hbm = pl.BlockSpec(memory_space=pltpu.HBM)
-    return pl.pallas_call(
+    early, last_scored, weights = pl.pallas_call(
         functools.partial(kernel, shuf_size, rep_size),
-        out_shape=pltpu.VMEM((block_rows, outs), bf16),
+        out_shape=(
+            pltpu.VMEM((block_rows - chunk, outs), bf16),
+            pltpu.VMEM((chunk, rep_size * cols), bf16),
+            pltpu.VMEM((2, half, slices, cols // slices, outs), bf16),
+        ),
         in_specs=[hbm, hbm, vmem, vmem, vmem, vmem],
-        out_specs=vmem,
+        out_specs=(vmem, vmem, vmem),
         scratch_shapes=[
             pltpu.VMEM((local_rows, cols), bf16),
             pltpu.VMEM((rep_size, block_rows, cols), bf16),
             pltpu.VMEM((2, outer, tiles + EXTRA, 2 * cols), f32),
-            pltpu.VMEM((2, half, slices, cols // slices, outs), bf16),
             pltpu.VMEM((rep_size, 2, tiles // rep_size, cols), f32),
             pltpu.VMEM((rep_size, 2, tiles // rep_size, cols), f32),
             pltpu.VMEM((chunk, rep_size * cols), bf16),
@@ -351,6 +380,14 @@
         col_gain[None, :],
         col_bias[None, :],
     )
+    return pl.pallas_call(
+        finish,
+        out_shape=jax.ShapeDtypeStruct((block_rows, outs), bf16),
+        in_specs=[vmem, vmem, vmem],
+        out_specs=hbm,
+        scratch_shapes=[pltpu.VMEM((chunk, outs), bf16), dma((CHUNKS,))],
+        compiler_params=pltpu.CompilerParams(vmem_limit_bytes=LIMIT_LAST),
+    )(early, last_scored, weights)
 
 
 def solution(mesh):

time: 59.1 us -> 58.4 us (0.988)
  local copies, waits for them, and re-layouts: 2.02 us -> 0 us
  Pallas kernels: 56.9 us -> 58.3 us
    pallas_call x0 -> x1, Pallas kernels: none -> 2.07 us  [on_device(): pl.pallas_call(finish, out_shape=jax.ShapeDtypeStruct((block_rows, outs),...]
    unnamed x1 -> x0, local copies, waits for them, and re-layouts: 2.02 us -> none
    pallas_call x1, Pallas kernels: 56.9 us -> 56.2 us  [on_device(): pl.pallas_call(functools.partial(kernel, shuf_size, rep_size), out_shape=...]
where the time goes in v3:
time: 58.4 us; the launch traced here: 58.3 us
  Pallas kernels  58.3 us (100%)
    pallas_call x1, Pallas kernels, on_device(): pl.pallas_call(functools.partial(kernel, shuf_size, rep_size), out_shape=...  56.2 us
    pallas_call x1, Pallas kernels, on_device(): pl.pallas_call(finish, out_shape=jax.ShapeDtypeStruct((block_rows, outs),...  2.07 us

profile of v3, /device:TPU:1, one launch (start us, length us, event | category | flops | bytes accessed | tf_op | source)
XLA Modules:
  0.0 58.3 jit_solution(12387454627463305367)
XLA Ops:
  0.0 56.2 %shard_map.64 = (bf16[1792,1024]{1,0:T(8,128)(2,1)S(1)}, bf16[256,1024]{1,0:T(8,128)(2,1)S(1)}, bf16[2,2,8,32,1024]{4,3,2,1,0:T(8,128)(2,1)S(1)}) custom-call(bf16[8192,256]{1,0:T(8,128)(2,1)} %values.1, bf16[8,32,1024]{2,1,0:T(8,128)(2,1)} %bitcast.5, s32[1,64]{1,0:T(1,128)} %bitcast.8, s32[1,64]{1,0:T(1,128)} %bitcast.9, f32[1,256]{1,0:T(1,128)} %bitcast.6, ...), custom_call_target="tpu_custom_call" | custom-call | tf_op jit(solution)/shard_map/pallas_call | solution.py:337
  56.2 2.1 %shard_map.65 = bf16[2048,1024]{1,0:T(8,128)(2,1)} custom-call(bf16[1792,1024]{1,0:T(8,128)(2,1)S(1)} %get-tuple-element.8.early, bf16[256,1024]{1,0:T(8,128)(2,1)S(1)} %get-tuple-element.9.scored, bf16[2,2,8,32,1024]{4,3,2,1,0:T(8,128)(2,1)S(1)} %get-tuple-element.10.weights), custom_call_target="tpu_custom_call" | custom-call | tf_op jit(solution)/shard_map/pallas_call | solution.py:383

commit v4 on v3

--- a/solution.py
+++ b/solution.py
@@ -38,6 +38,8 @@
     stats_out,
     stats_in,
     scored,
+    rep_ready,
+    shuf_ready,
     load_sem,
     own_sem,
     val_send,
@@ -114,11 +116,25 @@
     own_weight.start()
 
     barrier = pltpu.get_barrier_semaphore()
-    peers = [(shuf, rep_peer(dh, dl)) for dh, dl in rep_offsets]
-    peers += [(mate, rep)] + [(outer_peer(e), rep) for e in range(1, outer)]
-    for s, k in peers:
-        pl.semaphore_signal(barrier, inc=1, device_id=(s, k), device_id_type=MESH)
-    pl.semaphore_wait(barrier, len(peers))
+    leader, scout = low == 0, low == 1
+    for dh, dl in rep_offsets:
+        peer = rep_peer(dh, dl)
+
+        @pl.when(peer % half == 0)
+        def _():
+            pl.semaphore_signal(barrier, inc=1, device_id=(shuf, peer), device_id_type=MESH)
+
+    @pl.when(leader)
+    def _():
+        pl.semaphore_wait(barrier, rep_size - 1)
+        for dl in range(1, half):
+            pl.semaphore_signal(
+                rep_ready, inc=1, device_id=(shuf, rep_peer(0, dl)), device_id_type=MESH
+            )
+
+    @pl.when(jnp.logical_not(leader))
+    def _():
+        pl.semaphore_wait(rep_ready, 1)
 
     wx = remote(weight.at[cut], weights.at[1, 0, cut], wx_send, wx_recv, shuf, rep_peer(1, 0))
     wx.start()
@@ -130,6 +146,22 @@
     for ch in range(CHUNKS):
         for dh, dl in near:
             value_copy(dh, dl, ch).start()
+
+    shuf_peers = [mate] + [outer_peer(e) for e in range(1, outer)]
+
+    @pl.when(scout)
+    def _():
+        for s in shuf_peers:
+            pl.semaphore_signal(barrier, inc=1, device_id=(s, rep), device_id_type=MESH)
+        pl.semaphore_wait(barrier, len(shuf_peers))
+        for dl in range(1, half):
+            pl.semaphore_signal(
+                shuf_ready, inc=1, device_id=(shuf, rep_peer(0, dl)), device_id_type=MESH
+            )
+
+    @pl.when(jnp.logical_not(scout))
+    def _():
+        pl.semaphore_wait(shuf_ready, 1)
 
     gid_row = (owner[...] * GRP_DEV + member[...]).astype(jnp.float32)
     packets[0, 0, tiles:tiles + 1, :tiles] = gid_row
@@ -350,6 +382,8 @@
             pltpu.VMEM((rep_size, 2, tiles // rep_size, cols), f32),
             pltpu.VMEM((rep_size, 2, tiles // rep_size, cols), f32),
             pltpu.VMEM((chunk, rep_size * cols), bf16),
+            pltpu.SemaphoreType.REGULAR,
+            pltpu.SemaphoreType.REGULAR,
             dma((LOADS,)),
             dma,
             dma((rep_size, CHUNKS)),

time: 58.4 us -> 56.3 us (0.964)
  Pallas kernels: 58.3 us -> 55.7 us
    pallas_call x1, Pallas kernels: 56.2 us -> 53.6 us  [on_device(): pl.pallas_call(functools.partial(kernel, shuf_size, rep_size), out_shape=...]
where the time goes in v4:
time: 56.3 us; the launch traced here: 55.7 us
  Pallas kernels  55.7 us (99%)
    pallas_call x1, Pallas kernels, on_device(): pl.pallas_call(functools.partial(kernel, shuf_size, rep_size), out_shape=...  53.6 us
    pallas_call x1, Pallas kernels, on_device(): pl.pallas_call(finish, out_shape=jax.ShapeDtypeStruct((block_rows, outs),...  2.07 us

profile of v4, /device:TPU:1, one launch (start us, length us, event | category | flops | bytes accessed | tf_op | source)
XLA Modules:
  0.0 55.7 jit_solution(17236201338272289087)
XLA Ops:
  0.0 53.6 %shard_map.64 = (bf16[1792,1024]{1,0:T(8,128)(2,1)S(1)}, bf16[256,1024]{1,0:T(8,128)(2,1)S(1)}, bf16[2,2,8,32,1024]{4,3,2,1,0:T(8,128)(2,1)S(1)}) custom-call(bf16[8192,256]{1,0:T(8,128)(2,1)} %values.1, bf16[8,32,1024]{2,1,0:T(8,128)(2,1)} %bitcast.5, s32[1,64]{1,0:T(1,128)} %bitcast.8, s32[1,64]{1,0:T(1,128)} %bitcast.9, f32[1,256]{1,0:T(1,128)} %bitcast.6, ...), custom_call_target="tpu_custom_call" | custom-call | tf_op jit(solution)/shard_map/pallas_call | solution.py:369
  53.6 2.1 %shard_map.65 = bf16[2048,1024]{1,0:T(8,128)(2,1)} custom-call(bf16[1792,1024]{1,0:T(8,128)(2,1)S(1)} %get-tuple-element.8.early, bf16[256,1024]{1,0:T(8,128)(2,1)S(1)} %get-tuple-element.9.scored, bf16[2,2,8,32,1024]{4,3,2,1,0:T(8,128)(2,1)S(1)} %get-tuple-element.10.weights), custom_call_target="tpu_custom_call" | custom-call | tf_op jit(solution)/shard_map/pallas_call | solution.py:417
